TPU v7x, 32 devices: a whole 2x2x4 slice. The times are simulated.
32 devices in a mesh: fsdp: 4 (over z), context: 8 (over y, x, core).
Axes of the slice: x: 2, y: 2, z: 4, core: 2. Of those that a mesh axis runs over, the one named last changes fastest.
Arguments:
- block_input: bfloat16 [4, 1024, 1536], P('fsdp', 'context'), may hold values from -15 to 15
- cotangent: bfloat16 [4, 1024, 1536], P('fsdp', 'context'), may hold values from -6 to 6
- documents: int32 [4, 1024], P('fsdp', 'context'), may hold values from 0 to 7, as said below
- attn_weights: float32 [4608, 1536], P(('fsdp', 'context')), may hold values from -1.5 to 1.5
- ffn_weights: float32 [12288, 1536], P(('fsdp', 'context')), may hold values from -0.36 to 0.36
- norm_gains: float32 [2, 1536], replicated, may hold values from -0.5 to 0.5
- attn_moments: float32 [2, 4608, 1536], P(None, ('fsdp', 'context')), may hold values from -0.8 to 0.8, as said below
- ffn_moments: float32 [2, 12288, 1536], P(None, ('fsdp', 'context')), may hold values from -0.8 to 0.8, as said below
- gain_moments: float32 [2, 2, 1536], P(None, None, ('fsdp', 'context')), may hold values from -0.8 to 0.8, as said below
Outputs:
- block_output: float32 [4, 1024, 1536], P('fsdp', 'context')
- input_grad: float32 [4, 1024, 1536], P('fsdp', 'context')
- attn_grad: float32 [4608, 1536], P(('fsdp', 'context'))
- ffn_grad: float32 [12288, 1536], P(('fsdp', 'context'))
- gain_grad: float32 [2, 1536], P(None, ('fsdp', 'context'))
- new_attn_weights: float32 [4608, 1536], P(('fsdp', 'context'))
- new_ffn_weights: float32 [12288, 1536], P(('fsdp', 'context'))
- new_norm_gains: float32 [2, 1536], P(None, ('fsdp', 'context'))
- new_attn_moments: float32 [2, 4608, 1536], P(None, ('fsdp', 'context'))
- new_ffn_moments: float32 [2, 12288, 1536], P(None, ('fsdp', 'context'))
- new_gain_moments: float32 [2, 2, 1536], P(None, None, ('fsdp', 'context'))
Inputs may be any that keep to these rules, and one draw needn't show every extreme that they name: Segment numbers never fall along a sequence and start at 0; each sequence holds 8 documents of 50 to 640 tokens, one of exactly 640. `attn_moments`: entry 1 along the first dimension is positive. `ffn_moments`: entry 1 along the first dimension is positive. `gain_moments`: entry 1 along the first dimension is positive.
All inputs are finite; a program needn't handle non-finite values.
Results may differ from a plain program's by a relative error of at most 0.015.
Values may be sent and summed in bfloat16 or wider, within the bound.
A program may use at most 448 MiB of HBM per device.

v0:
```python
import math
import jax
import jax.numpy as jnp
from jax import lax
from jax.sharding import PartitionSpec as P

FF = 4096
QUERY_HEADS = 16
KEY_VALUE_HEADS = 8
HEAD_SIZE = 96
STEP = 3
NORM_EPS = 1e-05
ROPE_THETA = 100000.0
BETA_ONE = 0.9
BETA_TWO = 0.95
ADAM_EPS = 1e-08
LEARN_RATE = 0.02
WEIGHT_DECAY = 0.1


def product_transposed(left_matrix, right_matrix):
    return lax.dot_general(
        left_matrix, right_matrix, (((1,), (1,)), ((), ())), preferred_element_type=jnp.float32
    )


def transposed_times(left_matrix, right_matrix):
    return lax.dot_general(
        left_matrix, right_matrix, (((0,), (0,)), ((), ())), preferred_element_type=jnp.float32
    )


def plain_times(left_matrix, right_matrix):
    return jnp.dot(left_matrix, right_matrix, preferred_element_type=jnp.float32)


def rms_scale(tensor_in):
    return lax.rsqrt(jnp.mean(tensor_in * tensor_in, axis=-1, keepdims=True) + NORM_EPS)


def norm_backward(grad_in, normed, norm_scale, gain_row):
    scaled = grad_in * (1.0 + gain_row)
    return norm_scale * (scaled - normed * jnp.mean(scaled * normed, axis=-1, keepdims=True))


def rope_tables(positions):
    half_width = HEAD_SIZE // 2
    frequency = ROPE_THETA ** (-2.0 * jnp.arange(half_width, dtype=jnp.float32) / HEAD_SIZE)
    angles = positions.astype(jnp.float32)[:, None] * frequency[None, :]
    return (jnp.cos(angles), jnp.sin(angles))


def rotary_heads(tensor_in, cosine_lookup, sine_lookup, direction):
    half_width = HEAD_SIZE // 2
    first_half = tensor_in[..., :half_width]
    second_half = tensor_in[..., half_width:]
    cos_rows = cosine_lookup[:, None, :]
    sin_rows = sine_lookup[:, None, :] * direction
    return jnp.concatenate(
        [
            first_half * cos_rows - second_half * sin_rows,
            second_half * cos_rows + first_half * sin_rows,
        ],
        axis=-1,
    )


def split_weights(attn_full, ffn_full):
    query_width = QUERY_HEADS * HEAD_SIZE
    key_value_width = KEY_VALUE_HEADS * HEAD_SIZE
    return (
        attn_full[:query_width],
        attn_full[query_width : query_width + key_value_width],
        attn_full[query_width + key_value_width : query_width + 2 * key_value_width],
        attn_full[query_width + 2 * key_value_width :],
        ffn_full[:FF],
        ffn_full[FF : 2 * FF],
        ffn_full[2 * FF :],
    )


def adamw_update(parameter, gradient, moments, decay_rate):
    first_moment = BETA_ONE * moments[0] + (1.0 - BETA_ONE) * gradient
    second_moment = BETA_TWO * moments[1] + (1.0 - BETA_TWO) * gradient * gradient
    first_hat = first_moment / (1.0 - BETA_ONE**STEP)
    second_hat = second_moment / (1.0 - BETA_TWO**STEP)
    updated = parameter - LEARN_RATE * (
        first_hat / (jnp.sqrt(second_hat) + ADAM_EPS) + decay_rate * parameter
    )
    return (updated, jnp.stack([first_moment, second_moment]))


def on_device(
    block_input,
    cotangent,
    documents,
    attn_weights,
    ffn_weights,
    norm_gains,
    attn_moments,
    ffn_moments,
    gain_moments,
):
    local_rows = block_input.shape[1]
    heads_per_group = QUERY_HEADS // KEY_VALUE_HEADS
    query_width = QUERY_HEADS * HEAD_SIZE
    key_value_width = KEY_VALUE_HEADS * HEAD_SIZE
    score_scale = HEAD_SIZE ** (-0.5)
    grad_factor = float(local_rows * lax.axis_size(("fsdp", "context"))) ** (-0.5)
    attn_full, ffn_full = (
        lax.all_gather(attn_weights.astype(jnp.bfloat16), ("fsdp", "context"), axis=0, tiled=True),
        lax.all_gather(ffn_weights.astype(jnp.bfloat16), ("fsdp", "context"), axis=0, tiled=True),
    )
    w_query, key_weight, value_weight, w_out, w_gate, w_up, w_down = split_weights(
        attn_full, ffn_full
    )
    own_docs = documents[0]
    all_docs = lax.all_gather(own_docs, "context", axis=0, tiled=True)
    query_index = lax.axis_index("context") * local_rows + jnp.arange(local_rows, dtype=jnp.int32)
    doc_starts = jnp.sum((all_docs[None, :] < own_docs[:, None]).astype(jnp.int32), axis=1)
    cosine_lookup, sine_lookup = rope_tables(query_index - doc_starts)

    def block_mask(key_first, key_width):
        key_index = key_first + jnp.arange(key_width, dtype=jnp.int32)
        key_docs = lax.dynamic_slice_in_dim(all_docs, key_first, key_width, 0)
        return (key_index[None, :] <= query_index[:, None]) & (
            key_docs[None, :] == own_docs[:, None]
        )

    residual = block_input[0].astype(jnp.float32)
    scale_one = rms_scale(residual)
    normed_one = residual * scale_one
    first_hidden = (normed_one * (1.0 + norm_gains[0])).astype(jnp.bfloat16)
    query_matrix = rotary_heads(
        product_transposed(first_hidden, w_query).reshape(local_rows, QUERY_HEADS, HEAD_SIZE),
        cosine_lookup,
        sine_lookup,
        1.0,
    ).astype(jnp.bfloat16)
    key_flat = (
        rotary_heads(
            product_transposed(first_hidden, key_weight).reshape(
                local_rows, KEY_VALUE_HEADS, HEAD_SIZE
            ),
            cosine_lookup,
            sine_lookup,
            1.0,
        )
        .astype(jnp.bfloat16)
        .reshape(local_rows, key_value_width)
    )
    value_flat = product_transposed(first_hidden, value_weight).astype(jnp.bfloat16)
    grouped_queries = query_matrix.reshape(local_rows, KEY_VALUE_HEADS, heads_per_group, HEAD_SIZE)
    start_pair = (
        jnp.zeros((KEY_VALUE_HEADS, heads_per_group, local_rows, HEAD_SIZE), jnp.float32),
        jnp.zeros((KEY_VALUE_HEADS, heads_per_group, local_rows), jnp.float32),
    )
    key_piece = lax.all_gather(key_flat, "context", axis=0, tiled=True)
    value_piece = lax.all_gather(value_flat, "context", axis=0, tiled=True)
    piece_rows = key_piece.shape[0]
    inner_rows = math.gcd(piece_rows, 512)

    def sub_block(sub_index, inner_pair):
        out_sum, total_sum = inner_pair
        offset = sub_index * inner_rows
        key_block = lax.dynamic_slice_in_dim(key_piece, offset, inner_rows, 0).reshape(
            inner_rows, KEY_VALUE_HEADS, HEAD_SIZE
        )
        value_block = lax.dynamic_slice_in_dim(value_piece, offset, inner_rows, 0).reshape(
            inner_rows, KEY_VALUE_HEADS, HEAD_SIZE
        )
        allowed = block_mask(offset, inner_rows)
        scores = (
            jnp.einsum(
                "qhgd,khd->hgqk", grouped_queries, key_block, preferred_element_type=jnp.float32
            )
            * score_scale
        )
        exponent = jnp.where(allowed[None, None], jnp.exp(scores), 0.0)
        out_sum = out_sum + jnp.einsum(
            "hgqk,khd->hgqd",
            exponent.astype(jnp.bfloat16),
            value_block,
            preferred_element_type=jnp.float32,
        )
        return (out_sum, total_sum + jnp.sum(exponent, axis=-1))

    out_sum, totals = lax.fori_loop(0, piece_rows // inner_rows, sub_block, start_pair)
    log_totals = jnp.log(totals)
    attended_rows = (
        (out_sum / totals[..., None])
        .transpose(2, 0, 1, 3)
        .reshape(local_rows, query_width)
        .astype(jnp.bfloat16)
    )
    middle = residual + plain_times(attended_rows, w_out)
    scale_two = rms_scale(middle)
    normed_two = middle * scale_two
    hidden_two = (normed_two * (1.0 + norm_gains[1])).astype(jnp.bfloat16)
    gate_pre = product_transposed(hidden_two, w_gate)
    up_pre = product_transposed(hidden_two, w_up)
    sigmoid_gate = jax.nn.sigmoid(gate_pre)
    activated = (gate_pre * sigmoid_gate * up_pre).astype(jnp.bfloat16)
    block_out = middle + plain_times(activated, w_down)
    attn_back, ffn_back = (
        lax.all_gather(attn_weights.astype(jnp.bfloat16), ("fsdp", "context"), axis=0, tiled=True),
        lax.all_gather(ffn_weights.astype(jnp.bfloat16), ("fsdp", "context"), axis=0, tiled=True),
    )
    w_query, key_weight, value_weight, w_out, w_gate, w_up, w_down = split_weights(
        attn_back, ffn_back
    )
    seq_cotangent = cotangent[0]
    grad_act = product_transposed(seq_cotangent, w_down)
    grad_gate = (grad_act * up_pre * sigmoid_gate * (1.0 + gate_pre * (1.0 - sigmoid_gate))).astype(
        jnp.bfloat16
    )
    grad_up = (grad_act * gate_pre * sigmoid_gate).astype(jnp.bfloat16)
    ffn_term = (
        jnp.concatenate(
            [
                transposed_times(grad_gate, hidden_two),
                transposed_times(grad_up, hidden_two),
                transposed_times(activated, seq_cotangent),
            ],
            axis=0,
        )
        * grad_factor
    )
    grad_hidden_two = plain_times(grad_gate, w_gate) + plain_times(grad_up, w_up)
    gain_two = jnp.sum(grad_hidden_two * normed_two, axis=0)
    grad_middle = seq_cotangent.astype(jnp.float32) + norm_backward(
        grad_hidden_two, normed_two, scale_two, norm_gains[1]
    )
    grad_middle_bf = grad_middle.astype(jnp.bfloat16)
    grad_w_out = transposed_times(attended_rows, grad_middle_bf)
    attended_gradient = product_transposed(grad_middle_bf, w_out).astype(jnp.bfloat16)
    group_gradient = attended_gradient.reshape(
        local_rows, KEY_VALUE_HEADS, heads_per_group, HEAD_SIZE
    )
    row_delta = jnp.sum(
        group_gradient.astype(jnp.float32)
        * attended_rows.reshape(local_rows, KEY_VALUE_HEADS, heads_per_group, HEAD_SIZE).astype(
            jnp.float32
        ),
        axis=-1,
    ).transpose(1, 2, 0)
    seq_rows = local_rows * lax.axis_size("context")
    start_three = (
        jnp.zeros((KEY_VALUE_HEADS, heads_per_group, local_rows, HEAD_SIZE), jnp.float32),
        jnp.zeros((seq_rows, key_value_width), jnp.float32),
        jnp.zeros((seq_rows, key_value_width), jnp.float32),
    )
    attend_key_piece = lax.all_gather(key_flat, "context", axis=0, tiled=True)
    attend_value_piece = lax.all_gather(value_flat, "context", axis=0, tiled=True)
    piece_rows = attend_key_piece.shape[0]
    attend_inner_rows = math.gcd(piece_rows, 512)

    def sub_block(sub_index, inner_three):
        grad_query, grad_key_all, grad_value_all = inner_three
        offset = sub_index * attend_inner_rows
        key_block = lax.dynamic_slice_in_dim(
            attend_key_piece, offset, attend_inner_rows, 0
        ).reshape(attend_inner_rows, KEY_VALUE_HEADS, HEAD_SIZE)
        value_block = lax.dynamic_slice_in_dim(
            attend_value_piece, offset, attend_inner_rows, 0
        ).reshape(attend_inner_rows, KEY_VALUE_HEADS, HEAD_SIZE)
        allowed = block_mask(offset, attend_inner_rows)
        scores = (
            jnp.einsum(
                "qhgd,khd->hgqk", grouped_queries, key_block, preferred_element_type=jnp.float32
            )
            * score_scale
        )
        probabilities = jnp.where(allowed[None, None], jnp.exp(scores - log_totals[..., None]), 0.0)
        grad_probs = jnp.einsum(
            "qhgd,khd->hgqk", group_gradient, value_block, preferred_element_type=jnp.float32
        )
        grad_scores = (probabilities * (grad_probs - row_delta[..., None]) * score_scale).astype(
            jnp.bfloat16
        )
        grad_query = grad_query + jnp.einsum(
            "hgqk,khd->hgqd", grad_scores, key_block, preferred_element_type=jnp.float32
        )
        key_part = jnp.einsum(
            "hgqk,qhgd->khd", grad_scores, grouped_queries, preferred_element_type=jnp.float32
        ).reshape(attend_inner_rows, key_value_width)
        value_part = jnp.einsum(
            "hgqk,qhgd->khd",
            probabilities.astype(jnp.bfloat16),
            group_gradient,
            preferred_element_type=jnp.float32,
        ).reshape(attend_inner_rows, key_value_width)
        grad_key_all = lax.dynamic_update_slice_in_dim(grad_key_all, key_part, offset, 0)
        grad_value_all = lax.dynamic_update_slice_in_dim(grad_value_all, value_part, offset, 0)
        return (grad_query, grad_key_all, grad_value_all)

    grad_query_sum, grad_key_all, grad_value_all = lax.fori_loop(
        0, piece_rows // attend_inner_rows, sub_block, start_three
    )
    key_gradient_rows, grad_values = (
        lax.psum_scatter(
            grad_key_all.astype(jnp.bfloat16), "context", scatter_dimension=0, tiled=True
        ).astype(jnp.float32),
        lax.psum_scatter(
            grad_value_all.astype(jnp.bfloat16), "context", scatter_dimension=0, tiled=True
        ).astype(jnp.float32),
    )
    grad_q_bf = (
        rotary_heads(
            grad_query_sum.transpose(2, 0, 1, 3).reshape(local_rows, QUERY_HEADS, HEAD_SIZE),
            cosine_lookup,
            sine_lookup,
            -1.0,
        )
        .reshape(local_rows, query_width)
        .astype(jnp.bfloat16)
    )
    grad_k_bf = (
        rotary_heads(
            key_gradient_rows.reshape(local_rows, KEY_VALUE_HEADS, HEAD_SIZE),
            cosine_lookup,
            sine_lookup,
            -1.0,
        )
        .reshape(local_rows, key_value_width)
        .astype(jnp.bfloat16)
    )
    grad_v_bf = grad_values.astype(jnp.bfloat16)
    attn_term = (
        jnp.concatenate(
            [
                transposed_times(grad_q_bf, first_hidden),
                transposed_times(grad_k_bf, first_hidden),
                transposed_times(grad_v_bf, first_hidden),
                grad_w_out,
            ],
            axis=0,
        )
        * grad_factor
    )
    grad_hidden_one = (
        plain_times(grad_q_bf, w_query)
        + plain_times(grad_k_bf, key_weight)
        + plain_times(grad_v_bf, value_weight)
    )
    gain_one = jnp.sum(grad_hidden_one * normed_one, axis=0)
    grad_input = grad_middle + norm_backward(grad_hidden_one, normed_one, scale_one, norm_gains[0])
    gain_term = jnp.stack([gain_one, gain_two]) * grad_factor
    attn_shard, ffn_shard, gain_shard = (
        lax.psum_scatter(attn_term, ("fsdp", "context"), scatter_dimension=0, tiled=True),
        lax.psum_scatter(ffn_term, ("fsdp", "context"), scatter_dimension=0, tiled=True),
        lax.psum_scatter(gain_term, ("fsdp", "context"), scatter_dimension=1, tiled=True),
    )
    column_count = norm_gains.shape[1] // lax.axis_size(("fsdp", "context"))
    own_gains = lax.dynamic_slice_in_dim(
        norm_gains, lax.axis_index(("fsdp", "context")) * column_count, column_count, 1
    )
    new_attn, attn_states = adamw_update(attn_weights, attn_shard, attn_moments, WEIGHT_DECAY)
    new_ffn, ffn_states = adamw_update(ffn_weights, ffn_shard, ffn_moments, WEIGHT_DECAY)
    new_gains, gain_states = adamw_update(own_gains, gain_shard, gain_moments, 0.0)
    return (
        block_out[None],
        grad_input[None],
        attn_shard,
        ffn_shard,
        gain_shard,
        new_attn,
        new_ffn,
        new_gains,
        attn_states,
        ffn_states,
        gain_states,
    )


def solution(mesh):
    placed = (
        P("fsdp", "context", None),
        P("fsdp", "context", None),
        P("fsdp", "context"),
        P(("fsdp", "context"), None),
        P(("fsdp", "context"), None),
        P(),
        P(None, ("fsdp", "context"), None),
        P(None, ("fsdp", "context"), None),
        P(None, None, ("fsdp", "context")),
    )
    return jax.shard_map(
        on_device,
        mesh=mesh,
        in_specs=placed,
        out_specs=(
            P("fsdp", "context", None),
            P("fsdp", "context", None),
            P(("fsdp", "context"), None),
            P(("fsdp", "context"), None),
            P(None, ("fsdp", "context")),
            P(("fsdp", "context"), None),
            P(("fsdp", "context"), None),
            P(None, ("fsdp", "context")),
            P(None, ("fsdp", "context"), None),
            P(None, ("fsdp", "context"), None),
            P(None, None, ("fsdp", "context")),
        ),
        check_vma=False,
    )
```

profile of v0, /device:TPU:0, one launch (start us, length us, event | category | flops | bytes accessed | tf_op | source)
XLA Modules:
  0.0 1589.9 jit_solution(6565524639662273563)
XLA Ops:
  11.3 105.4 %all-gather.6.cloned.1.call-done = bf16[4608,1536]{1,0:T(8,128)(2,1)} async-done(((bf16[144,1536]{1,0:T(8,128)(2,1)}), bf16[4608,1536]{1,0:T(8,128)(2,1)}) %all-gather.6.cloned.1.call-update) | async-done | bytes 14155792 | tf_op jit(solution)/shard_map/all_gather | solution.py:111
  116.7 3.5 fusion.65
  120.3 8.7 all-gather
  138.1 6.3 all-gather.10.cloned.1.call-done
  147.0 25.7 %all-gather.8.cloned.1.call-done = bf16[1024,768]{0,1:T(8,128)(2,1)} async-done(((bf16[128,768]{0,1:T(8,128)(2,1)}), bf16[1024,768]{0,1:T(8,128)(2,1)}) %all-gather.8.cloned.1.call-update) | async-done | bytes 1572880 | tf_op jit(solution)/shard_map/all_gather | solution.py:158
  172.7 16.3 %while.34 = (s32[]{:T(128)}, f32[8,2,128,96]{2,3,1,0:T(8,128)S(1)}, f32[8,2,128]{2,1,0:T(2,128)S(1)}, s32[1024]{0:T(1024)S(1)}, s32[1,128]{1,0:T(1,128)S(1)}, /*...) while((s32[]{:T(128)}, f32[8,2,128,96]{2,3,1,0:T(8,128)S(1)}, ...), condition=%wide.region_4.5_spmd.clone, body=%wide.region_2.4_spmd.clone.sunk | while | flops 409537152 | bytes 15314638 | solution.py:188
  177.5 3.1 fusion.177
  185.5 3.4 fusion.177
  189.1 3.4 multiply_reduce_fusion.3
  192.6 197.7 %all-gather.12.cloned.1.call-done = bf16[12288,1536]{1,0:T(8,128)(2,1)} async-done(((bf16[384,1536]{1,0:T(8,128)(2,1)}), bf16[12288,1536]{1,0:T(8,128)(2,1)}) %all-gather.12.cloned.1.call-update) | async-done | bytes 37748752 | tf_op jit(solution)/shard_map/all_gather | solution.py:112
  390.4 7.0 fusion.30
  397.4 7.1 fusion.36
  404.5 8.4 multiply_convert_fusion.1
  412.9 6.4 fusion.34
  419.4 6.1 multiply_reduce_fusion
  433.4 28.3 %while.35 = (s32[]{:T(128)}, f32[8,2,128,96]{2,3,1,0:T(8,128)}, bf16[1024,768]{0,1:T(8,128)(2,1)}, bf16[1024,768]{0,1:T(8,128)(2,1)}, s32[1024]{0:T(1024)S(1)}, ...) while((s32[]{:T(128)}, f32[8,2,128,96]{2,3,1,0:T(8,128)}, ...), condition=%wide.region_9.10_spmd.clone, body=%wide.region_8.9_spmd.clone.sunk | while | flops 1018757760 | bytes 91197336 | solution.py:297
  466.3 3.3 fusion.114
  469.6 5.0 fusion.96
  474.6 4.9 fusion.99
  479.6 21.5 %reduce-scatter.16.cloned.1.call-done = bf16[128,768]{1,0:T(8,128)(2,1)} async-done(((bf16[1024,768]{1,0:T(8,128)(2,1)}), bf16[128,768]{1,0:T(8,128)(2,1)}) %reduce-scatter.16.cloned.1.call-update) | async-done | bytes 196624
  507.5 35.7 %reduce-scatter.18.cloned.1.call-done = bf16[128,768]{1,0:T(8,128)(2,1)} async-done(((bf16[1024,768]{1,0:T(8,128)(2,1)}), bf16[128,768]{1,0:T(8,128)(2,1)}) %reduce-scatter.18.cloned.1.call-update) | async-done | bytes 196624
  543.2 3.2 fusion.81
  550.1 18.1 %maximum_multiply_fusion.1 = f32[4608,1536]{1,0:T(8,128)} fusion(f32[1536,1536]{1,0:T(8,128)} %fusion.99, f32[768,1536]{1,0:T(8,128)S(1)} %fusion.103, f32[768,1536]{1,0:T(8,128)S(1)} %copy-done.5, f32[1536,1536]{1,0:T(8,128)} %fusion.96), kind=kLoop, calls=%fused_computation.42 | loop fusion | flops 28311552 | bytes 56623104 | tf_op jit(solution)/shard_map/mul | solution.py:330
  569.1 11.5 fusion.119
  580.7 10.2 fusion.118
  590.9 10.2 fusion.87
  601.0 51.5 %maximum_multiply_fusion = f32[12288,1536]{1,0:T(8,128)} fusion(f32[4096,1536]{1,0:T(8,128)} %fusion.87, f32[4096,1536]{1,0:T(8,128)} %fusion.119, f32[4096,1536]{1,0:T(8,128)} %fusion.118), kind=kLoop, calls=%fused_computation.41 | loop fusion | flops 56623104 | bytes 150994944 | tf_op jit(solution)/shard_map/mul | solution.py:219
  653.7 8.5 fusion.55
  666.1 248.1 %reduce-scatter.12.cloned.1.call-done = f32[144,1536]{1,0:T(8,128)} async-done(((f32[4608,1536]{1,0:T(8,128)}), f32[144,1536]{1,0:T(8,128)}) %reduce-scatter.12.cloned.1.call-update) | async-done | bytes 884752 | tf_op jit(solution)/shard_map/reduce_scatter | solution.py:350
  914.2 3.3 fusion.98
  918.8 655.4 %reduce-scatter.14.cloned.1.call-done = f32[384,1536]{1,0:T(8,128)} async-done(((f32[12288,1536]{1,0:T(8,128)}), f32[384,1536]{1,0:T(8,128)}) %reduce-scatter.14.cloned.1.call-update) | async-done | bytes 2359312 | tf_op jit(solution)/shard_map/reduce_scatter | solution.py:351
  1574.2 6.3 fusion.85
  (198 shorter events, 85.6 us)
Async XLA Ops:
  7.2 113.1 %copy-start.29 = (s32[1,128]{1,0:T(1,128)S(1)}, s32[1,128]{1,0:T(1,128)}, u32[]{:S(2)}) copy-start(s32[1,128]{1,0:T(1,128)} %param.15) | copy-start | bytes 1540
  7.2 109.5 %all-gather.6.cloned.1.call-start = ((), (), s32[]{:S(2)}) async-start(), calls=%async_computation.5 | async-start | bytes 14598144 | tf_op jit(solution)/shard_map/all_gather | solution.py:111
  9.2 135.2 %all-gather.10.cloned.1.call-start = ((), (), s32[]{:S(2)}) async-start(), calls=%async_computation.7 | async-start | bytes 1769472 | tf_op jit(solution)/shard_map/all_gather | solution.py:159
  116.7 12.8 slice-start.4
  116.7 12.8 copy-start.3
  120.3 52.4 %all-gather.8.cloned.1.call-start = ((), (), s32[]{:S(2)}) async-start(), calls=%async_computation.6 | async-start | bytes 1769472 | tf_op jit(solution)/shard_map/all_gather | solution.py:158
  131.1 259.3 %all-gather.12.cloned.1.call-start = ((), (), s32[]{:S(2)}) async-start(), calls=%async_computation.8 | async-start | bytes 38928384 | tf_op jit(solution)/shard_map/all_gather | solution.py:112
  134.0 367.1 %reduce-scatter.16.cloned.1.call-start = ((), (), s32[]{:S(2)}) async-start(), calls=%async_computation.11 | async-start | bytes 1769472
  189.0 201.4 %copy-start.21 = (bf16[1,128,1536]{2,1,0:T(8,128)(2,1)S(1)}, bf16[1,128,1536]{2,1,0:T(8,128)(2,1)}, u32[]{:S(2)}) copy-start(bf16[1,128,1536]{2,1,0:T(8,128)(2,1)} %param.14) | copy-start | bytes 1179652
  192.5 226.9 %copy-start.17 = (f32[128,1536]{1,0:T(8,128)}, f32[128,1536]{1,0:T(8,128)S(1)}, u32[]{:S(2)}) copy-start(f32[128,1536]{1,0:T(8,128)S(1)} %get-tuple-element.633) | copy-start | bytes 2359300
  192.6 211.9 %copy-start.15 = (bf16[128,1536]{1,0:T(8,128)(2,1)}, bf16[128,1536]{1,0:T(8,128)(2,1)S(1)}, u32[]{:S(2)}) copy-start(bf16[128,1536]{1,0:T(8,128)(2,1)S(1)} %multiply_convert_fusion.3) | copy-start | bytes 1179652
  412.9 6.4 copy-start.26
  412.9 6.5 copy-start.24
  412.9 14.0 slice-start
  412.9 14.0 slice-start.1
  419.4 7.6 slice-start.2
  419.4 7.6 slice-start.3
  449.5 4.7 copy-start
  464.4 78.8 %reduce-scatter.18.cloned.1.call-start = ((), (), s32[]{:S(2)}) async-start(), calls=%async_computation.12 | async-start | bytes 1769472
  466.2 197.1 %reduce-scatter.20.cloned.1.call-start = ((), (), s32[]{:S(2)}) async-start(), calls=%async_computation.13 | async-start | bytes 811008
  469.6 5.1 copy-start.8
  469.6 5.1 copy-start.20
  547.7 366.5 %reduce-scatter.12.cloned.1.call-start = ((), (), s32[]{:S(2)}) async-start(), calls=%async_computation.9 | async-start | bytes 29196288 | tf_op jit(solution)/shard_map/reduce_scatter | solution.py:350
  568.1 12.5 copy-start.25
  568.1 1006.1 %reduce-scatter.14.cloned.1.call-start = ((), (), s32[]{:S(2)}) async-start(), calls=%async_computation.10 | async-start | bytes 77856768 | tf_op jit(solution)/shard_map/reduce_scatter | solution.py:351
  580.7 10.2 copy-start.22
  580.7 10.2 copy-start.23
  653.7 8.5 copy-start.27
  653.7 10.5 copy-start.31
  653.7 260.5 %copy-start.14 = (f32[144,1536]{1,0:T(8,128)S(1)}, f32[144,1536]{1,0:T(8,128)}, u32[]{:S(2)}) copy-start(f32[144,1536]{1,0:T(8,128)} %param.16) | copy-start | bytes 2654212
  664.2 254.6 %copy-start.30 = (f32[2,48]{1,0:T(2,128)}, f32[2,48]{1,0:T(2,128)S(1)}, u32[]{:S(2)}) copy-start(f32[2,48]{1,0:T(2,128)S(1)} %copy.64) | copy-start | bytes 1156
  666.1 908.1 %copy-start.6 = (f32[384,1536]{1,0:T(8,128)S(1)}, f32[384,1536]{1,0:T(8,128)}, u32[]{:S(2)}) copy-start(f32[384,1536]{1,0:T(8,128)} %param.17) | copy-start | bytes 7077892
  (21 other events, 55.9 us)
Sparse Core Ops, SparseCore 0:
  11.5 105.2 all-gather.5
  120.4 23.9 all-gather.9
  146.9 25.7 all-gather.7
  176.0 214.3 all-gather.11
  464.5 36.5 reduce-scatter.15
  504.8 38.3 reduce-scatter.17
  548.9 96.1 reduce-scatter.19
  652.1 262.0 reduce-scatter.11
  921.2 653.0 reduce-scatter.13
where the time goes:
time: 1600 us; the launch traced here: 1590 us
  waiting for transfers between devices  1300 us (81%)
  matrix products  138 us (9%)
  other arithmetic  98 us (6%)
  local copies, waits for them, and re-layouts  33.7 us (2%)
    reduce_scatter x1, waiting for transfers between devices, on_device(): lax.psum_scatter(ffn_term, ('fsdp', 'context'), scatter_dimension=0, tile...  655 us
    reduce_scatter x1, waiting for transfers between devices, on_device(): lax.psum_scatter(attn_term, ('fsdp', 'context'), scatter_dimension=0, til...  248 us
    all_gather x1, waiting for transfers between devices, on_device(): lax.all_gather(ffn_weights.astype(jnp.bfloat16), ('fsdp', 'context'), axi...  198 us
    all_gather x1, waiting for transfers between devices, on_device(): lax.all_gather(attn_weights.astype(jnp.bfloat16), ('fsdp', 'context'), ax...  105 us
    unnamed x12, waiting for transfers between devices  57.3 us
    mul x1, other arithmetic, on_device(): jnp.concatenate([transposed_times(grad_gate, hidden_two), transposed_time...  51.5 us
    dot_general x7, matrix products, transposed_times(): lax.dot_general(left_matrix, right_matrix, (((0,), (0,)), ((), ())), pref...  45.8 us
    dot_general x7, matrix products, plain_times(): jnp.dot(left_matrix, right_matrix, preferred_element_type=jnp.float32)  33 us
  transfers between devices with their start and end apart: 9, of which 8 were waited for; matrix products, arithmetic and copies ran while one was open for 11% of the time, Pallas kernels for 0%

commit v1 on v0

--- a/solution.py
+++ b/solution.py
@@ -107,8 +107,26 @@
     key_value_width = KEY_VALUE_HEADS * HEAD_SIZE
     score_scale = HEAD_SIZE ** (-0.5)
     grad_factor = float(local_rows * lax.axis_size(("fsdp", "context"))) ** (-0.5)
+
+    def feed_shifts_all(field, ax_name):
+        then = lax.axis_size(ax_name)
+        before = lax.axis_index(ax_name)
+        y_new, outer = (then, before)
+        mixed_arr, answer = (field, 1)
+        while answer < y_new:
+            y2 = lax.ppermute(
+                mixed_arr,
+                axis_name=ax_name,
+                perm=[(src_i, src_i ^ answer) for src_i in range(y_new)],
+            )
+            w2 = jnp.concatenate([mixed_arr, y2], 0)
+            carry = jnp.concatenate([y2, mixed_arr], 0)
+            mixed_arr = jnp.where(outer & answer == 0, w2, carry)
+            answer = 2 * answer
+        return mixed_arr
+
     attn_full, ffn_full = (
-        lax.all_gather(attn_weights.astype(jnp.bfloat16), ("fsdp", "context"), axis=0, tiled=True),
+        feed_shifts_all(attn_weights.astype(jnp.bfloat16), ("fsdp", "context")),
         lax.all_gather(ffn_weights.astype(jnp.bfloat16), ("fsdp", "context"), axis=0, tiled=True),
     )
     w_query, key_weight, value_weight, w_out, w_gate, w_up, w_down = split_weights(

time: 1600 us -> 2040 us (1.27)
  waiting for transfers between devices: 1300 us -> 1700 us
  other arithmetic: 98 us -> 120 us
    ppermute x0 -> x5, waiting for transfers between devices: none -> 438 us  [feed_shifts_all(): lax.ppermute(mixed_arr, axis_name=ax_name, perm=[(src_i, src_i ^ answer)...]
    all_gather x1, waiting for transfers between devices: 105 us -> 68.4 us  [on_device(): lax.all_gather(attn_weights.astype(jnp.bfloat16), ('fsdp', 'context'), ax...]
    select_n x0 -> x5, other arithmetic: none -> 26.1 us  [feed_shifts_all(): mixed_arr = jnp.where(outer & answer == 0, w2, carry)]
  transfers between devices with their start and end apart: 9 -> 14, of which waited for: 8 -> 13; matrix products, arithmetic and copies ran while one was open for 11% -> 10% of each run, Pallas kernels for 0% -> 0%
where the time goes in v1:
time: 2040 us; the launch traced here: 2030 us
  waiting for transfers between devices  1700 us (83%)
  matrix products  138 us (7%)
  other arithmetic  120 us (6%)
  local copies, waits for them, and re-layouts  38.7 us (2%)
    reduce_scatter x1, waiting for transfers between devices, on_device(): lax.psum_scatter(ffn_term, ('fsdp', 'context'), scatter_dimension=0, tile...  656 us
    ppermute x5, waiting for transfers between devices, feed_shifts_all(): lax.ppermute(mixed_arr, axis_name=ax_name, perm=[(src_i, src_i ^ answer)...  438 us
    reduce_scatter x1, waiting for transfers between devices, on_device(): lax.psum_scatter(attn_term, ('fsdp', 'context'), scatter_dimension=0, til...  248 us
    all_gather x1, waiting for transfers between devices, on_device(): lax.all_gather(ffn_weights.astype(jnp.bfloat16), ('fsdp', 'context'), axi...  198 us
    all_gather x1, waiting for transfers between devices, on_device(): lax.all_gather(attn_weights.astype(jnp.bfloat16), ('fsdp', 'context'), ax...  68.4 us
    unnamed x12, waiting for transfers between devices  58.1 us
    mul x1, other arithmetic, on_device(): jnp.concatenate([transposed_times(grad_gate, hidden_two), transposed_time...  51.4 us
    dot_general x7, matrix products, transposed_times(): lax.dot_general(left_matrix, right_matrix, (((0,), (0,)), ((), ())), pref...  45.8 us
  transfers between devices with their start and end apart: 14, of which 13 were waited for; matrix products, arithmetic and copies ran while one was open for 10% of the time, Pallas kernels for 0%

profile of v1, /device:TPU:0, one launch (start us, length us, event | category | flops | bytes accessed | tf_op | source)
XLA Modules:
  0.0 2030.8 jit_solution(17074950280520263205)
XLA Ops:
  13.6 20.1 collective-permute-done.1
  37.5 38.4 %collective-permute-done.2 = bf16[576,1536]{1,0:T(8,128)(2,1)} collective-permute-done((bf16[576,1536]{1,0:T(8,128)(2,1)S(1)}, bf16[576,1536]{1,0:T(8,128)(2,1)}, u32[]{:S(2)}, u32[]{:S(2)}) %collective-permute-start.2) | collective-permute-done | bytes 1769504 | tf_op jit(solution)/shard_map/ppermute | solution.py:117
  81.2 75.9 %collective-permute-done.3 = bf16[1152,1536]{1,0:T(8,128)(2,1)} collective-permute-done((bf16[1152,1536]{1,0:T(8,128)(2,1)}, bf16[1152,1536]{1,0:T(8,128)(2,1)}, u32[]{:S(2)}, u32[]{:S(2)}) %collective-permute-start.3) | collective-permute-done | bytes 3538976 | tf_op jit(solution)/shard_map/ppermute | solution.py:117
  157.1 8.7 maximum_select_fusion.1
  168.3 302.5 %collective-permute-done.4 = bf16[2304,1536]{1,0:T(8,128)(2,1)} collective-permute-done((bf16[2304,1536]{1,0:T(8,128)(2,1)}, bf16[2304,1536]{1,0:T(8,128)(2,1)}, u32[]{:S(2)}, u32[]{:S(2)}) %collective-permute-start.4) | collective-permute-done | bytes 7077920 | tf_op jit(solution)/shard_map/ppermute | solution.py:117
  470.9 11.3 maximum_select_fusion
  482.2 5.0 copy-done.2
  488.9 8.3 all-gather
  507.3 7.8 all-gather.8.cloned.1.call-done
  517.7 25.7 %all-gather.6.cloned.1.call-done = bf16[1024,768]{0,1:T(8,128)(2,1)} async-done(((bf16[128,768]{0,1:T(8,128)(2,1)}), bf16[1024,768]{0,1:T(8,128)(2,1)}) %all-gather.6.cloned.1.call-update) | async-done | bytes 1572880 | tf_op jit(solution)/shard_map/all_gather | solution.py:176
  543.4 16.3 while.34
  563.4 197.9 %all-gather.10.cloned.1.call-done = bf16[12288,1536]{1,0:T(8,128)(2,1)} async-done(((bf16[384,1536]{1,0:T(8,128)(2,1)}), bf16[12288,1536]{1,0:T(8,128)(2,1)}) %all-gather.10.cloned.1.call-update) | async-done | bytes 37748752 | tf_op jit(solution)/shard_map/all_gather | solution.py:130
  761.3 7.0 fusion.30
  768.3 7.2 fusion.36
  775.5 8.4 multiply_convert_fusion.1
  784.0 6.4 fusion.34
  790.4 6.2 multiply_reduce_fusion
  796.9 68.4 %all-gather.12.cloned.1.call-done = bf16[4608,1536]{1,0:T(8,128)(2,1)} async-done(((bf16[144,1536]{1,0:T(8,128)(2,1)}), bf16[4608,1536]{1,0:T(8,128)(2,1)}) %all-gather.12.cloned.1.call-update) | async-done | bytes 14155792 | tf_op jit(solution)/shard_map/all_gather | solution.py:224
  874.0 28.3 %while.35 = (s32[]{:T(128)}, f32[8,2,128,96]{2,3,1,0:T(8,128)}, bf16[1024,768]{0,1:T(8,128)(2,1)}, bf16[1024,768]{0,1:T(8,128)(2,1)}, s32[1024]{0:T(1024)S(1)}, ...) while((s32[]{:T(128)}, f32[8,2,128,96]{2,3,1,0:T(8,128)}, ...), condition=%wide.region_9.10_spmd.clone, body=%wide.region_8.9_spmd.clone.sunk | while | flops 1018757760 | bytes 91197336 | solution.py:315
  910.2 5.0 fusion.99
  915.2 4.9 fusion.102
  920.1 21.8 %reduce-scatter.16.cloned.1.call-done = bf16[128,768]{1,0:T(8,128)(2,1)} async-done(((bf16[1024,768]{1,0:T(8,128)(2,1)}), bf16[128,768]{1,0:T(8,128)(2,1)}) %reduce-scatter.16.cloned.1.call-update) | async-done | bytes 196624
  948.4 35.6 %reduce-scatter.18.cloned.1.call-done = bf16[128,768]{1,0:T(8,128)(2,1)} async-done(((bf16[1024,768]{1,0:T(8,128)(2,1)}), bf16[128,768]{1,0:T(8,128)(2,1)}) %reduce-scatter.18.cloned.1.call-update) | async-done | bytes 196624
  990.9 17.9 maximum_multiply_fusion.1
  1009.8 11.6 fusion.119
  1021.4 10.2 fusion.118
  1031.6 10.2 fusion.90
  1041.7 51.4 %maximum_multiply_fusion = f32[12288,1536]{1,0:T(8,128)} fusion(f32[4096,1536]{1,0:T(8,128)} %fusion.90, f32[4096,1536]{1,0:T(8,128)} %fusion.119, f32[4096,1536]{1,0:T(8,128)} %fusion.118), kind=kLoop, calls=%fused_computation.41 | loop fusion | flops 56623104 | bytes 150994944 | tf_op jit(solution)/shard_map/mul | solution.py:237
  1094.3 8.3 fusion.57
  1106.5 248.5 %reduce-scatter.12.cloned.1.call-done = f32[144,1536]{1,0:T(8,128)} async-done(((f32[4608,1536]{1,0:T(8,128)}), f32[144,1536]{1,0:T(8,128)}) %reduce-scatter.12.cloned.1.call-update) | async-done | bytes 884752 | tf_op jit(solution)/shard_map/reduce_scatter | solution.py:368
  1359.6 655.6 %reduce-scatter.14.cloned.1.call-done = f32[384,1536]{1,0:T(8,128)} async-done(((f32[12288,1536]{1,0:T(8,128)}), f32[384,1536]{1,0:T(8,128)}) %reduce-scatter.14.cloned.1.call-update) | async-done | bytes 2359312 | tf_op jit(solution)/shard_map/reduce_scatter | solution.py:369
  2015.3 6.3 fusion.88
  (212 shorter events, 123.0 us)
Async XLA Ops:
  7.2 508.0 %all-gather.8.cloned.1.call-start = ((), (), s32[]{:S(2)}) async-start(), calls=%async_computation.6 | async-start | bytes 1769472 | tf_op jit(solution)/shard_map/all_gather | solution.py:177
  8.4 71.2 %copy-start.15 = (bf16[144,1536]{1,0:T(8,128)(2,1)}, bf16[144,1536]{1,0:T(8,128)(2,1)S(1)}, u32[]{:S(2)}) copy-start(bf16[144,1536]{1,0:T(8,128)(2,1)S(1)} %convert_element_type.151) | copy-start | bytes 1327108
  8.5 2.0 collective-permute-start
  10.6 23.0 %collective-permute-start.1 = (bf16[288,1536]{1,0:T(8,128)(2,1)S(1)}, bf16[288,1536]{1,0:T(8,128)(2,1)}, u32[]{:S(2)}, u32[]{:S(2)}) collective-permute-start(bf16[288,1536]{1,0:T(8,128)(2,1)S(1)} %maximum_select_fusion.4), channel_id=1, source_target_pairs={{0,2},{1,3},{2,0},{3,1},{4,6},{5,7},{6,4},{7,5},{8,10},{9,11},{10,... | collective-permute-start | bytes 2654216 | tf_op jit(solution)/shard_map/ppermute | solution.py:117
  35.7 40.2 %collective-permute-start.2 = (bf16[576,1536]{1,0:T(8,128)(2,1)S(1)}, bf16[576,1536]{1,0:T(8,128)(2,1)}, u32[]{:S(2)}, u32[]{:S(2)}) collective-permute-start(bf16[576,1536]{1,0:T(8,128)(2,1)S(1)} %maximum_select_fusion.3), channel_id=1, source_target_pairs={{0,4},{1,5},{2,6},{3,7},{4,0},{5,1},{6,2},{7,3},{8,12},{9,13},{10,... | collective-permute-start | bytes 5308424 | tf_op jit(solution)/shard_map/ppermute | solution.py:117
  79.7 77.5 %collective-permute-start.3 = (bf16[1152,1536]{1,0:T(8,128)(2,1)}, bf16[1152,1536]{1,0:T(8,128)(2,1)}, u32[]{:S(2)}, u32[]{:S(2)}) collective-permute-start(bf16[1152,1536]{1,0:T(8,128)(2,1)} %maximum_select_fusion.2), channel_id=1, source_target_pairs={{0,8},{1,9},{2,10},{3,11},{4,12},{5,13},{6,14},{7,15},{8,0},{9,1},... | collective-permute-start | bytes 10616840 | tf_op jit(solution)/shard_map/ppermute | solution.py:117
  81.2 86.9 %copy-start.33 = (f32[2,1536]{1,0:T(2,128)S(1)}, f32[2,1536]{1,0:T(2,128)}, u32[]{:S(2)}) copy-start(f32[2,1536]{1,0:T(2,128)} %param.18) | copy-start | bytes 36868
  81.2 86.9 %copy-start.4 = (bf16[1,128,1536]{2,1,0:T(8,128)(2,1)S(1)}, bf16[1,128,1536]{2,1,0:T(8,128)(2,1)}, u32[]{:S(2)}) copy-start(bf16[1,128,1536]{2,1,0:T(8,128)(2,1)} %param.13) | copy-start | bytes 1179652
  165.8 305.0 %collective-permute-start.4 = (bf16[2304,1536]{1,0:T(8,128)(2,1)}, bf16[2304,1536]{1,0:T(8,128)(2,1)}, u32[]{:S(2)}, u32[]{:S(2)}) collective-permute-start(bf16[2304,1536]{1,0:T(8,128)(2,1)} %maximum_select_fusion.1), channel_id=1, source_target_pairs={{0,16},{1,17},{2,18},{3,19},{4,20},{5,21},{6,22},{7,23},{8,24},{9,... | collective-permute-start | bytes 21233672 | tf_op jit(solution)/shard_map/ppermute | solution.py:117
  168.3 320.6 %copy-start.32 = (s32[1,128]{1,0:T(1,128)S(1)}, s32[1,128]{1,0:T(1,128)}, u32[]{:S(2)}) copy-start(s32[1,128]{1,0:T(1,128)} %param.15) | copy-start | bytes 1540
  488.8 8.8 slice-start
  488.9 54.5 %all-gather.6.cloned.1.call-start = ((), (), s32[]{:S(2)}) async-start(), calls=%async_computation.5 | async-start | bytes 1769472 | tf_op jit(solution)/shard_map/all_gather | solution.py:176
  499.3 261.9 %all-gather.10.cloned.1.call-start = ((), (), s32[]{:S(2)}) async-start(), calls=%async_computation.7 | async-start | bytes 38928384 | tf_op jit(solution)/shard_map/all_gather | solution.py:130
  502.2 363.1 %all-gather.12.cloned.1.call-start = ((), (), s32[]{:S(2)}) async-start(), calls=%async_computation.8 | async-start | bytes 14598144 | tf_op jit(solution)/shard_map/all_gather | solution.py:224
  502.8 439.2 %reduce-scatter.16.cloned.1.call-start = ((), (), s32[]{:S(2)}) async-start(), calls=%async_computation.11 | async-start | bytes 1769472
  559.7 201.5 %copy-start.23 = (bf16[1,128,1536]{2,1,0:T(8,128)(2,1)S(1)}, bf16[1,128,1536]{2,1,0:T(8,128)(2,1)}, u32[]{:S(2)}) copy-start(bf16[1,128,1536]{2,1,0:T(8,128)(2,1)} %param.14) | copy-start | bytes 1179652
  563.2 233.4 %copy-start.19 = (f32[128,1536]{1,0:T(8,128)}, f32[128,1536]{1,0:T(8,128)S(1)}, u32[]{:S(2)}) copy-start(f32[128,1536]{1,0:T(8,128)S(1)} %get-tuple-element.633) | copy-start | bytes 2359300
  563.4 212.1 %copy-start.17 = (bf16[128,1536]{1,0:T(8,128)(2,1)}, bf16[128,1536]{1,0:T(8,128)(2,1)S(1)}, u32[]{:S(2)}) copy-start(bf16[128,1536]{1,0:T(8,128)(2,1)S(1)} %multiply_convert_fusion.3) | copy-start | bytes 1179652
  784.0 6.4 copy-start.27
  796.9 74.4 %copy-start.8 = (f32[128,1536]{1,0:T(8,128)}, f32[128,1536]{1,0:T(8,128)S(1)}, u32[]{:S(2)}) copy-start(f32[128,1536]{1,0:T(8,128)S(1)} %multiply_add_fusion) | copy-start | bytes 2359300
  905.0 79.0 %reduce-scatter.18.cloned.1.call-start = ((), (), s32[]{:S(2)}) async-start(), calls=%async_computation.12 | async-start | bytes 1769472
  906.9 196.9 %reduce-scatter.20.cloned.1.call-start = ((), (), s32[]{:S(2)}) async-start(), calls=%async_computation.13 | async-start | bytes 811008
  988.5 366.5 %reduce-scatter.12.cloned.1.call-start = ((), (), s32[]{:S(2)}) async-start(), calls=%async_computation.9 | async-start | bytes 29196288 | tf_op jit(solution)/shard_map/reduce_scatter | solution.py:368
  1008.8 12.5 copy-start.28
  1008.8 1006.4 %reduce-scatter.14.cloned.1.call-start = ((), (), s32[]{:S(2)}) async-start(), calls=%async_computation.10 | async-start | bytes 77856768 | tf_op jit(solution)/shard_map/reduce_scatter | solution.py:369
  1021.4 10.2 copy-start.25
  1021.4 10.2 copy-start.26
  1094.3 8.3 copy-start.30
  1094.3 10.3 copy-start.35
  1094.3 260.7 %copy-start.16 = (f32[144,1536]{1,0:T(8,128)S(1)}, f32[144,1536]{1,0:T(8,128)}, u32[]{:S(2)}) copy-start(f32[144,1536]{1,0:T(8,128)} %param.16) | copy-start | bytes 2654212
  1104.6 255.0 %copy-start.34 = (f32[2,48]{1,0:T(2,128)}, f32[2,48]{1,0:T(2,128)S(1)}, u32[]{:S(2)}) copy-start(f32[2,48]{1,0:T(2,128)S(1)} %copy.64) | copy-start | bytes 1156
  1106.5 908.8 %copy-start.7 = (f32[384,1536]{1,0:T(8,128)S(1)}, f32[384,1536]{1,0:T(8,128)}, u32[]{:S(2)}) copy-start(f32[384,1536]{1,0:T(8,128)} %param.17) | copy-start | bytes 7077892
  (26 other events, 84.7 us)
Sparse Core Ops, SparseCore 0:
  489.0 26.1 all-gather.7
  517.6 25.7 all-gather.5
  546.9 214.3 all-gather.9
  764.6 100.6 all-gather.11
  905.1 36.7 reduce-scatter.15
  945.7 38.3 reduce-scatter.17
  989.7 96.2 reduce-scatter.19
  1093.0 261.9 reduce-scatter.11
  1362.0 653.2 reduce-scatter.13
